TPU v7x, 32 devices: a whole 2x2x4 slice. The times are simulated.
32 devices in a mesh: ep: 8 (over z, y), dp: 4 (over x, core).
Axes of the slice: x: 2, y: 2, z: 4, core: 2. Of those that a mesh axis runs over, the one named last changes fastest.
Arguments:
- tokens: bfloat16 [6144, 2880], P(('ep', 'dp')), may hold values from -64 to 64
- out_grad: bfloat16 [6144, 2880], P(('ep', 'dp')), may hold values from -6 to 6
- indices: int32 [6144, 4], P(('ep', 'dp')), may hold values from 0 to 31, as said below
- expert_rows: bfloat16 [4, 32, 8, 36, 2880], P('dp', 'ep'), may hold values from -0.111328125 to 0.111328125
- router_weight: bfloat16 [2880, 32], replicated, may hold values from -1 to 1
- router_bias: float32 [32], replicated, may hold values from -3 to 3
- balance_scale: float32 [1], replicated, may hold values from 64 to 256
Outputs:
- token_grad: bfloat16 [6144, 2880], P(('ep', 'dp'))
- weight_grad: float32 [2880, 32], P('dp', 'ep')
- balance_loss: float32 [1], replicated
Inputs may be any that keep to these rules, and one draw needn't show every extreme that they name: `indices`: each row names 4 different experts. Within the 192 rows of one device no expert is named by more than 36 rows, and some expert is named by exactly 36 rows. Within the rows of one device the 4 experts of one ep index (experts j * 4 to j * 4 + 3) are named by at most 108 rows together, and those of some ep index by exactly 108. Every expert is named by some row of every device.
All inputs are finite; a program needn't handle non-finite values.
Results may differ from a plain program's by a relative error of at most 0.0014.
The roundings to bfloat16 on the way count: a program that leaves them out, or rounds other values in their place, can miss the bound.
Values may be sent and summed in bfloat16 or wider, within the bound.
No kernel may reach another device: no remote copies, remote signals or barrier semaphores. Data moves between devices by JAX's collectives and lax.ppermute only.
A program may use at most 128 MiB of HBM per device.

v0:
```python
import math
import jax
import jax.numpy as jnp
from jax import lax
from jax.sharding import PartitionSpec as P


def on_device(tokens, out_grad, indices, expert_rows, router_weight, router_bias, balance_scale):
    tok_dev = tokens.shape[0]
    chosen = indices.shape[1]
    width = tokens.shape[1]
    experts = router_weight.shape[1]
    capacity = expert_rows.shape[3]
    ep_size = lax.axis_size("ep")
    dp_size = lax.axis_size("dp")
    token_total = tok_dev * ep_size * dp_size
    expert_ids = jnp.arange(experts, dtype=jnp.int32)
    onehot = (indices[:, :, None] == expert_ids[None, None, :]).astype(jnp.float32)
    named_by = jnp.sum(onehot, axis=1)
    local_counts = jnp.sum(named_by, axis=0)
    logits = jnp.dot(tokens, router_weight, preferred_element_type=jnp.float32) + router_bias
    probability = jax.nn.softmax(logits, axis=-1)
    counts, prob_sums = lax.psum((local_counts, jnp.sum(probability, axis=0)), ("ep", "dp"))
    share_of = counts / (token_total * chosen)
    balance_loss = (experts * jnp.sum(share_of * (prob_sums / token_total))).reshape(1)
    row_ids = jnp.arange(tok_dev, dtype=jnp.int32)
    lower_mask = (row_ids[:, None] > row_ids[None, :]).astype(jnp.bfloat16)
    before = jnp.dot(lower_mask, named_by.astype(jnp.bfloat16), preferred_element_type=jnp.float32)
    slot_index = jnp.sum(onehot * before[:, None, :], axis=2).astype(jnp.int32)
    returned = lax.all_to_all(expert_rows, "ep", split_axis=2, concat_axis=1, tiled=True)
    flat_rows = returned.reshape(experts * capacity, width)
    row_index = indices * capacity + slot_index
    picked = jnp.take(flat_rows, row_index, axis=0)
    pair_dots = jnp.einsum("td,tkd->tk", out_grad, picked, preferred_element_type=jnp.float32)
    chosen_logits = jnp.take_along_axis(logits, indices, axis=1)
    mix_weight = jax.nn.softmax(chosen_logits, axis=-1)
    sel_grad = mix_weight * (pair_dots - jnp.sum(mix_weight * pair_dots, axis=1, keepdims=True))
    balance_push = balance_scale[0] * experts * share_of
    spread = probability * (
        balance_push[None, :] - jnp.sum(probability * balance_push[None, :], axis=1, keepdims=True)
    )
    logit_grad = (spread + jnp.sum(onehot * sel_grad[:, :, None], axis=1)).astype(jnp.bfloat16)
    token_grad = lax.dot_general(
        logit_grad, router_weight, (((1,), (1,)), ((), ())), preferred_element_type=jnp.float32
    ).astype(jnp.bfloat16)
    term = lax.dot_general(
        tokens, logit_grad, (((0,), (0,)), ((), ())), preferred_element_type=jnp.float32
    )
    summed = lax.psum_scatter(term, "ep", scatter_dimension=1, tiled=True)
    summed = lax.psum_scatter(summed, "dp", scatter_dimension=0, tiled=True)
    weight_grad = summed / math.sqrt(token_total)
    return (token_grad, weight_grad, balance_loss)


def solution(mesh):
    placed = (
        P(("ep", "dp"), None),
        P(("ep", "dp"), None),
        P(("ep", "dp"), None),
        P("dp", "ep", None, None, None),
        P(),
        P(),
        P(),
    )
    return jax.shard_map(
        on_device,
        mesh=mesh,
        in_specs=placed,
        out_specs=(P(("ep", "dp"), None), P("dp", "ep"), P()),
        check_vma=False,
    )
```

profile of v0, /device:TPU:0, one launch (start us, length us, event | category | flops | bytes accessed | tf_op | source)
XLA Modules:
  0.0 366.3 jit_solution(14106931418418347998)
XLA Ops:
  7.2 7.0 %copy.48 = bf16[1,4,8,36,2880]{4,3,1,0,2:T(8,128)(2,1)} copy(bf16[1,4,8,36,2880]{4,2,3,1,0:T(8,128)(2,1)} %param.10) | data formatting | bytes 13271040 | tf_op args[3]
  14.2 7.5 %all-to-all-start = ((bf16[1,4,8,36,2880]{4,3,1,0,2:T(8,128)(2,1)}), bf16[1,4,8,36,2880]{4,3,1,0,2:T(8,128)(2,1)}, u32[]{:S(2)}, u32[]{:S(2)}) async-start(bf16[1,4,8,36,2880]{4,3,1,0,2:T(8,128)(2,1)} %copy.48), calls=%async_computation | async-start | bytes 15073280 | tf_op jit(solution)/shard_map/all_to_all | solution.py:30
  21.8 0.1 fusion.5
  21.9 0.2 convert_reduce_fusion.1
  22.1 184.7 %psum.14 = f32[32]{0:T(128)S(1)} all-reduce(f32[32]{0:T(128)S(1)} %get-tuple-element.5), channel_id=1, replica_groups=mesh['ep'=8,'dp'=4] {'ep','dp'}, use_global_device_ids=true, to_apply=%region_3.0 | all-reduce | flops 32 | bytes 256 | tf_op jit(solution)/shard_map/psum | solution.py:23
  206.8 0.1 copy.49
  206.9 0.1 reshape.45
  207.0 0.2 copy.47
  207.2 0.1 copy.45
  207.3 0.1 reshape.51
  207.4 0.5 fusion.16
  207.9 6.3 %gather_fusion.1 = f32[768]{0:T(1024)S(1)} fusion(f32[192,32]{0,1:T(8,128)S(1)} %get-tuple-element.12, s32[768]{0:T(1024)S(1)} %reshape.51), kind=kCustom, calls=%fused_computation.1 | custom fusion | bytes 12288 | tf_op jit(solution)/shard_map/jit(take_along_axis)/gather | solution.py:35
  214.3 0.1 reshape.54
  214.4 0.1 copy.46
  215.2 0.1 fusion.14
  215.4 9.3 %reshape.41 = bf16[1152,2880]{1,0:T(8,128)(2,1)} reshape(bf16[1,8,4,1,36,2880]{5,4,2,1,3,0:T(8,128)(2,1)} %bitcast.3) | data formatting | bytes 13271040 | tf_op jit(solution)/shard_map/reshape | solution.py:31
  224.7 13.1 %gather_fusion = bf16[768,2880]{1,0:T(8,128)(2,1)} fusion(bf16[1152,2880]{1,0:T(8,128)(2,1)} %reshape.41, s32[1024]{0:T(1024)S(1)} %pad_clamp_fusion), kind=kCustom, calls=%fused_computation | custom fusion | bytes 8850432 | tf_op jit(solution)/shard_map/jit(_take)/gather | solution.py:33
  237.8 7.1 %reshape.44 = bf16[192,4,2880]{2,1,0:T(4,128)(2,1)} reshape(bf16[768,2880]{1,0:T(8,128)(2,1)} %gather_fusion) | data formatting | bytes 8847360 | tf_op jit(solution)/shard_map/jit(_take)/gather | solution.py:33
  244.9 9.4 %fusion = f32[192,1,4]{2,1,0:T(1,128)S(1)} fusion(bf16[192,4,2880]{2,1,0:T(4,128)(2,1)} %reshape.44, pred[192,4]{1,0:T(8,128)(4,1)S(1)} %copy.47, bf16[192,2880,1]{1,0,2:T(8,128)(2,1)S(1)} %bitcast.30), kind=kOutput, calls=%fused_computation.2 | convolution fusion | flops 6635520 | bytes 5533440 | tf_op jit(solution)/shard_map/td,tkd->tk/dot_general | solution.py:34
  254.3 0.1 copy.51
  254.5 0.1 add_convert_fusion
  254.6 1.1 convolution_bitcast_fusion
  255.7 39.3 %psum.15 = f32[32]{0:T(128)S(1)} all-reduce(f32[32]{0:T(128)S(1)} %get-tuple-element.3), channel_id=1, replica_groups=mesh['ep'=8,'dp'=4] {'ep','dp'}, use_global_device_ids=true, to_apply=%region_14.15 | all-reduce | flops 32 | bytes 256 | tf_op jit(solution)/shard_map/psum | solution.py:23
  295.0 0.6 dynamic-slice
  296.3 0.6 multiply_reduce_fusion.1
  297.5 29.8 %all-reduce.3.cloned.1.call-done = f32[2880,32]{0,1:T(8,128)} async-done(((f32[2880,32]{0,1:T(8,128)}), f32[2880,32]{0,1:T(8,128)}) %all-reduce.3.cloned.1.call-update) | async-done | bytes 368656
  327.3 0.9 constant_dynamic-slice_fusion
  328.2 1.6 copy.52
  329.9 1.5 convolution_convert_fusion
  331.4 25.2 %reduce-scatter.4.cloned.1.call-done = f32[720,4]{1,0:T(8,128)} async-done(((f32[2880,4]{1,0:T(8,128)}), f32[720,4]{1,0:T(8,128)}) %reduce-scatter.4.cloned.1.call-update) | async-done | bytes 11536
  356.6 1.1 copy.53
  357.7 0.6 broadcast_multiply_fusion
  (28 shorter events, 0.3 us)
Async XLA Ops:
  7.2 237.8 %copy-start = (bf16[192,2880]{1,0:T(8,128)(2,1)S(1)}, bf16[192,2880]{1,0:T(8,128)(2,1)}, u32[]{:S(2)}) copy-start(bf16[192,2880]{1,0:T(8,128)(2,1)} %param.8) | copy-start | bytes 3317764
  14.2 7.5 %copy-start.3 = (s32[192,4]{0,1:T(4,128)S(1)}, s32[192,4]{0,1:T(4,128)}, u32[]{:S(2)}) copy-start(s32[192,4]{0,1:T(4,128)} %param.9) | copy-start | bytes 9220
  14.2 193.2 %copy-start.1 = (bf16[192,2880]{1,0:T(8,128)(2,1)S(1)}, bf16[192,2880]{1,0:T(8,128)(2,1)}, u32[]{:S(2)}) copy-start(bf16[192,2880]{1,0:T(8,128)(2,1)} %param.7) | copy-start | bytes 3317764
  14.2 193.2 %copy-start.2 = (bf16[2880,32]{0,1:T(8,128)(2,1)S(1)}, bf16[2880,32]{0,1:T(8,128)(2,1)}, u32[]{:S(2)}) copy-start(bf16[2880,32]{0,1:T(8,128)(2,1)} %param.11) | copy-start | bytes 552964
  14.2 193.2 %copy-start.4 = (f32[32]{0:T(128)S(1)}, f32[32]{0:T(128)}, u32[]{:S(2)}) copy-start(f32[32]{0:T(128)} %param.12) | copy-start | bytes 388
  14.2 201.1 %all-to-all-start = ((bf16[1,4,8,36,2880]{4,3,1,0,2:T(8,128)(2,1)}), bf16[1,4,8,36,2880]{4,3,1,0,2:T(8,128)(2,1)}, u32[]{:S(2)}, u32[]{:S(2)}) async-start(bf16[1,4,8,36,2880]{4,3,1,0,2:T(8,128)(2,1)} %copy.48), calls=%async_computation | async-start | bytes 15073280 | tf_op jit(solution)/shard_map/all_to_all | solution.py:30
  21.7 305.6 %all-reduce.3.cloned.1.call-start = ((), (), s32[]{:S(2)}) async-start(), calls=%async_computation.3 | async-start | bytes 753664
  244.9 50.1 %copy-start.5 = (u32[32]{0:T(128)S(1)}, u32[32]{0:T(128)}, u32[]{:S(2)}) copy-start(u32[32]{0:T(128)} %constant.70) | copy-start | bytes 388
  255.7 100.9 %reduce-scatter.4.cloned.1.call-start = ((), (), s32[]{:S(2)}) async-start(), calls=%async_computation.2 | async-start | bytes 1843200
Sparse Core Ops, SparseCore 0:
  255.8 71.4 all-reduce.2
  330.0 26.5 reduce-scatter.3
where the time goes:
time: 367 us; the launch traced here: 366 us
  blocking collectives  224 us (61%)
  waiting for transfers between devices  55.1 us (15%)
  local copies, waits for them, and re-layouts  48.1 us (13%)
  between operations  17.3 us (5%)
  matrix products  12.6 us (3%)
  starting transfers between devices  7.53 us (2%)
    psum x2, blocking collectives, on_device(): lax.psum((local_counts, jnp.sum(probability, axis=0)), ('ep', 'dp'))  224 us
    unnamed x4, waiting for transfers between devices  55.1 us
    gather x2, local copies, waits for them, and re-layouts, on_device(): picked = jnp.take(flat_rows, row_index, axis=0)  20.2 us
    unnamed x17, local copies, waits for them, and re-layouts  11.3 us
    dot_general x1, matrix products, on_device(): jnp.einsum('td,tkd->tk', out_grad, picked, preferred_element_type=jnp.flo...  9.4 us
    reshape x1, local copies, waits for them, and re-layouts, on_device(): flat_rows = returned.reshape(experts * capacity, width)  9.32 us
    all_to_all x1, starting transfers between devices, on_device(): lax.all_to_all(expert_rows, 'ep', split_axis=2, concat_axis=1, tiled=True)  7.45 us
  transfers between devices with their start and end apart: 3, of which 2 were waited for; matrix products, arithmetic and copies ran while one was open for 3% of the time, Pallas kernels for 0%

commit v1 on v0

--- a/solution.py
+++ b/solution.py
@@ -20,7 +20,7 @@
     local_counts = jnp.sum(named_by, axis=0)
     logits = jnp.dot(tokens, router_weight, preferred_element_type=jnp.float32) + router_bias
     probability = jax.nn.softmax(logits, axis=-1)
-    counts, prob_sums = lax.psum((local_counts, jnp.sum(probability, axis=0)), ("ep", "dp"))
+    counts, prob_sums = lax.psum(lax.psum((local_counts, jnp.sum(probability, axis=0)), "dp"), "ep")
     share_of = counts / (token_total * chosen)
     balance_loss = (experts * jnp.sum(share_of * (prob_sums / token_total))).reshape(1)
     row_ids = jnp.arange(tok_dev, dtype=jnp.int32)

time: 367 us -> 346 us (0.943)
  blocking collectives: 224 us -> 173 us
  waiting for transfers between devices: 55.1 us -> 85.3 us
    psum x2 -> x4, blocking collectives: 224 us -> 173 us  [the longest x2 160 us: on_device(): lax.psum(lax.psum((local_counts, jnp.sum(probability, axis=0)), 'dp'), 'ep')]
    all_to_all x1, waiting for transfers between devices: 0.01 us -> 16.9 us  [on_device(): lax.all_to_all(expert_rows, 'ep', split_axis=2, concat_axis=1, tiled=True)]
    unnamed x4, waiting for transfers between devices: 55.1 us -> 68.4 us
  transfers between devices with their start and end apart: 3 -> 3, of which waited for: 2 -> 3; matrix products, arithmetic and copies ran while one was open for 3% -> 3% of each run, Pallas kernels for 0% -> 0%
where the time goes in v1:
time: 346 us; the launch traced here: 345 us
  blocking collectives  173 us (50%)
  waiting for transfers between devices  85.3 us (25%)
  local copies, waits for them, and re-layouts  48.1 us (14%)
  between operations  17.3 us (5%)
  matrix products  12.6 us (4%)
  starting transfers between devices  7.53 us (2%)
    psum x2, blocking collectives, on_device(): lax.psum(lax.psum((local_counts, jnp.sum(probability, axis=0)), 'dp'), 'ep')  160 us
    unnamed x4, waiting for transfers between devices  68.4 us
    gather x2, local copies, waits for them, and re-layouts, on_device(): picked = jnp.take(flat_rows, row_index, axis=0)  20.2 us
    all_to_all x1, waiting for transfers between devices, on_device(): lax.all_to_all(expert_rows, 'ep', split_axis=2, concat_axis=1, tiled=True)  16.9 us
    psum x2, blocking collectives, on_device(): lax.psum((local_counts, jnp.sum(probability, axis=0)), 'dp')  12.4 us
    unnamed x17, local copies, waits for them, and re-layouts  11.3 us
    dot_general x1, matrix products, on_device(): jnp.einsum('td,tkd->tk', out_grad, picked, preferred_element_type=jnp.flo...  9.4 us
    reshape x1, local copies, waits for them, and re-layouts, on_device(): flat_rows = returned.reshape(experts * capacity, width)  9.31 us
  transfers between devices with their start and end apart: 3, of which 3 were waited for; matrix products, arithmetic and copies ran while one was open for 3% of the time, Pallas kernels for 0%

profile of v1, /device:TPU:0, one launch (start us, length us, event | category | flops | bytes accessed | tf_op | source)
XLA Modules:
  0.0 345.3 jit_solution(11753358687123654903)
XLA Ops:
  7.2 7.0 %copy.48 = bf16[1,4,8,36,2880]{4,3,1,0,2:T(8,128)(2,1)} copy(bf16[1,4,8,36,2880]{4,2,3,1,0:T(8,128)(2,1)} %param.10) | data formatting | bytes 13271040 | tf_op args[3]
  14.2 7.5 %all-to-all-start = ((bf16[1,4,8,36,2880]{4,3,1,0,2:T(8,128)(2,1)}), bf16[1,4,8,36,2880]{4,3,1,0,2:T(8,128)(2,1)}, u32[]{:S(2)}, u32[]{:S(2)}) async-start(bf16[1,4,8,36,2880]{4,3,1,0,2:T(8,128)(2,1)} %copy.48), calls=%async_computation | async-start | bytes 15073280 | tf_op jit(solution)/shard_map/all_to_all | solution.py:30
  21.8 0.1 fusion.5
  21.9 0.2 convert_reduce_fusion.1
  22.1 0.1 copy.49
  22.2 0.1 reshape.45
  22.3 0.2 copy.47
  22.5 0.1 copy.45
  22.6 0.1 reshape.51
  22.8 0.5 fusion.16
  23.3 6.3 %gather_fusion.1 = f32[768]{0:T(1024)S(1)} fusion(f32[192,32]{0,1:T(8,128)S(1)} %get-tuple-element.12, s32[768]{0:T(1024)S(1)} %reshape.51), kind=kCustom, calls=%fused_computation.1 | custom fusion | bytes 12288 | tf_op jit(solution)/shard_map/jit(take_along_axis)/gather | solution.py:35
  29.6 0.1 reshape.54
  30.5 6.7 %psum.28 = f32[32]{0:T(128)S(1)} all-reduce(f32[32]{0:T(128)S(1)} %get-tuple-element.5), channel_id=1, replica_groups=mesh['ep'=8,'dp'=4] {'dp'}, use_global_device_ids=true, to_apply=%region_3.0 | all-reduce | flops 32 | bytes 256 | tf_op jit(solution)/shard_map/psum | solution.py:23
  37.2 132.4 %psum.29 = f32[32]{0:T(128)S(1)} all-reduce(f32[32]{0:T(128)S(1)} %psum.28), channel_id=1, replica_groups=mesh['ep'=8,'dp'=4] {'ep'}, use_global_device_ids=true, to_apply=%region_4.0 | all-reduce | flops 32 | bytes 256 | tf_op jit(solution)/shard_map/psum | solution.py:23
  169.7 0.1 fusion.14
  169.8 16.9 %all-to-all-done = bf16[1,4,8,36,2880]{4,3,1,0,2:T(8,128)(2,1)} async-done(((bf16[1,4,8,36,2880]{4,3,1,0,2:T(8,128)(2,1)}), bf16[1,4,8,36,2880]{4,3,1,0,2:T(8,128)(2,1)}, u32[]{:S(2)}, u32[]{:S(2)}) %all-to-all-start) | async-done | bytes 6635552 | tf_op jit(solution)/shard_map/all_to_all | solution.py:30
  186.7 9.3 %reshape.41 = bf16[1152,2880]{1,0:T(8,128)(2,1)} reshape(bf16[1,8,4,1,36,2880]{5,4,2,1,3,0:T(8,128)(2,1)} %bitcast.3) | data formatting | bytes 13271040 | tf_op jit(solution)/shard_map/reshape | solution.py:31
  196.0 13.1 %gather_fusion = bf16[768,2880]{1,0:T(8,128)(2,1)} fusion(bf16[1152,2880]{1,0:T(8,128)(2,1)} %reshape.41, s32[1024]{0:T(1024)S(1)} %pad_clamp_fusion), kind=kCustom, calls=%fused_computation | custom fusion | bytes 8850432 | tf_op jit(solution)/shard_map/jit(_take)/gather | solution.py:33
  209.1 7.1 %reshape.44 = bf16[192,4,2880]{2,1,0:T(4,128)(2,1)} reshape(bf16[768,2880]{1,0:T(8,128)(2,1)} %gather_fusion) | data formatting | bytes 8847360 | tf_op jit(solution)/shard_map/jit(_take)/gather | solution.py:33
  216.2 9.4 %fusion = f32[192,1,4]{2,1,0:T(1,128)S(1)} fusion(bf16[192,4,2880]{2,1,0:T(4,128)(2,1)} %reshape.44, pred[192,4]{1,0:T(8,128)(4,1)S(1)} %copy.47, bf16[192,2880,1]{1,0,2:T(8,128)(2,1)S(1)} %bitcast.30), kind=kOutput, calls=%fused_computation.2 | convolution fusion | flops 6635520 | bytes 5533440 | tf_op jit(solution)/shard_map/td,tkd->tk/dot_general | solution.py:34
  225.9 1.1 convolution_bitcast_fusion
  227.1 0.6 dynamic-slice
  228.3 5.7 %psum.30 = f32[32]{0:T(128)S(1)} all-reduce(f32[32]{0:T(128)S(1)} %get-tuple-element.3), channel_id=1, replica_groups=mesh['ep'=8,'dp'=4] {'dp'}, use_global_device_ids=true, to_apply=%region_15.16 | all-reduce | flops 32 | bytes 256 | tf_op jit(solution)/shard_map/psum | solution.py:23
  234.0 27.9 %psum.31 = f32[32]{0:T(128)S(1)} all-reduce(f32[32]{0:T(128)S(1)} %psum.30), channel_id=1, replica_groups=mesh['ep'=8,'dp'=4] {'ep'}, use_global_device_ids=true, to_apply=%region_16.17 | all-reduce | flops 32 | bytes 256 | tf_op jit(solution)/shard_map/psum | solution.py:23
  261.9 0.6 multiply_reduce_fusion.1
  263.1 43.1 %all-reduce.3.cloned.1.call-done = f32[2880,32]{0,1:T(8,128)} async-done(((f32[2880,32]{0,1:T(8,128)}), f32[2880,32]{0,1:T(8,128)}) %all-reduce.3.cloned.1.call-update) | async-done | bytes 368656
  306.3 0.9 constant_dynamic-slice_fusion
  307.2 1.6 copy.52
  308.8 1.5 convolution_convert_fusion
  310.3 25.2 %reduce-scatter.4.cloned.1.call-done = f32[720,4]{1,0:T(8,128)} async-done(((f32[2880,4]{1,0:T(8,128)}), f32[720,4]{1,0:T(8,128)}) %reduce-scatter.4.cloned.1.call-update) | async-done | bytes 11536
  335.5 1.1 copy.53
  336.7 0.6 broadcast_multiply_fusion
  (30 shorter events, 0.6 us)
Async XLA Ops:
  7.2 209.1 %copy-start = (bf16[192,2880]{1,0:T(8,128)(2,1)S(1)}, bf16[192,2880]{1,0:T(8,128)(2,1)}, u32[]{:S(2)}) copy-start(bf16[192,2880]{1,0:T(8,128)(2,1)} %param.8) | copy-start | bytes 3317764
  14.2 7.5 %copy-start.3 = (s32[192,4]{0,1:T(4,128)S(1)}, s32[192,4]{0,1:T(4,128)}, u32[]{:S(2)}) copy-start(s32[192,4]{0,1:T(4,128)} %param.9) | copy-start | bytes 9220
  14.2 8.5 %copy-start.1 = (bf16[192,2880]{1,0:T(8,128)(2,1)S(1)}, bf16[192,2880]{1,0:T(8,128)(2,1)}, u32[]{:S(2)}) copy-start(bf16[192,2880]{1,0:T(8,128)(2,1)} %param.7) | copy-start | bytes 3317764
  14.2 8.5 %copy-start.2 = (bf16[2880,32]{0,1:T(8,128)(2,1)S(1)}, bf16[2880,32]{0,1:T(8,128)(2,1)}, u32[]{:S(2)}) copy-start(bf16[2880,32]{0,1:T(8,128)(2,1)} %param.11) | copy-start | bytes 552964
  14.2 8.5 %copy-start.4 = (f32[32]{0:T(128)S(1)}, f32[32]{0:T(128)}, u32[]{:S(2)}) copy-start(f32[32]{0:T(128)} %param.12) | copy-start | bytes 388
  14.2 172.5 %all-to-all-start = ((bf16[1,4,8,36,2880]{4,3,1,0,2:T(8,128)(2,1)}), bf16[1,4,8,36,2880]{4,3,1,0,2:T(8,128)(2,1)}, u32[]{:S(2)}, u32[]{:S(2)}) async-start(bf16[1,4,8,36,2880]{4,3,1,0,2:T(8,128)(2,1)} %copy.48), calls=%async_computation | async-start | bytes 15073280 | tf_op jit(solution)/shard_map/all_to_all | solution.py:30
  21.7 284.6 %all-reduce.3.cloned.1.call-start = ((), (), s32[]{:S(2)}) async-start(), calls=%async_computation.3 | async-start | bytes 753664
  216.2 10.8 %copy-start.5 = (u32[32]{0:T(128)S(1)}, u32[32]{0:T(128)}, u32[]{:S(2)}) copy-start(u32[32]{0:T(128)} %constant.70) | copy-start | bytes 388
  227.0 108.5 %reduce-scatter.4.cloned.1.call-start = ((), (), s32[]{:S(2)}) async-start(), calls=%async_computation.2 | async-start | bytes 1843200
Sparse Core Ops, SparseCore 0:
  227.1 79.0 all-reduce.2
  308.9 26.5 reduce-scatter.3
